TPU v7x, 32 devices: a whole 2x2x4 slice. The times are simulated.
32 devices in a mesh: grid: 8 (over y, x, core), rows: 4 (over z).
Axes of the slice: x: 2, y: 2, z: 4, core: 2. Of those that a mesh axis runs over, the one named last changes fastest.
Arguments:
- density: bfloat16 [32, 128, 4096], P(None, 'rows', 'grid'), as said below
- basis_values: bfloat16 [16, 16, 128, 512], P('grid', None, 'rows'), may hold values from -0.59765625 to 0.59765625
- grid_points: float32 [16, 3, 512], P('grid'), may hold values from -4 to 4
- grid_weights: float32 [16, 512], P('grid'), may hold values from 0.05 to 1
- screened_blocks: int32 [16, 16], P('grid'), may hold values from 0 to 31, as said below
Outputs:
- exchange: float32 [32, 128, 4096], P(None, 'rows', 'grid')
Inputs may be any that keep to these rules, and one draw needn't show every extreme that they name: density is symmetric: density[a, i, b * 128 + j] equals density[b, j, a * 128 + i]. `screened_blocks`: each row holds 16 distinct block numbers.
All inputs are finite; a program needn't handle non-finite values.
Results may differ from a plain program's by a relative error of at most 0.00055.
The roundings to bfloat16 on the way count: a program that leaves them out, or rounds other values in their place, can miss the bound.
Values may be sent and summed in bfloat16 or wider, within the bound.
A program may use at most 128 MiB of HBM per device.

v0:
```python
import jax
import jax.numpy as jnp
from jax import lax
from jax.sharding import PartitionSpec as P


def body(density, basis_values, grid_points, grid_weights, screened_blocks):
    nblocks = density.shape[0]
    rows_mine = density.shape[1]
    block_size = rows_mine * lax.axis_size("rows")
    nbasis = nblocks * block_size
    nsig = basis_values.shape[1]
    npoints = basis_values.shape[3]
    stripe = lax.all_gather(density, "grid", axis=2, tiled=True)
    totals = jnp.zeros((nblocks, rows_mine, nblocks, block_size), jnp.float32)
    for batch_index in range(basis_values.shape[0]):
        blocks = screened_blocks[batch_index]
        row_pick = jnp.take(stripe, blocks, axis=0).reshape(nsig * rows_mine, nblocks, block_size)
        chosen = jnp.take(row_pick, blocks, axis=1)
        local_values = basis_values[batch_index]
        x_mine = local_values.reshape(nsig * rows_mine, npoints)
        fsum = jnp.einsum(
            "mtk,tkp->mp",
            chosen,
            lax.all_gather(local_values, "rows", axis=1, tiled=True),
            preferred_element_type=jnp.float32,
        )
        fmat = fsum.astype(jnp.bfloat16)
        intersection_part = lax.dot_general(
            x_mine, fmat, (((0,), (0,)), ((), ())), preferred_element_type=jnp.float32
        )
        intersection = lax.psum(intersection_part, "rows")
        places = grid_points[batch_index]
        weights = grid_weights[batch_index]
        diffs = places[:, :, None] - places[:, None, :]
        kern = 1.0 / jnp.sqrt(jnp.sum(diffs * diffs, axis=0) + 0.5)
        mixed = (weights[:, None] * kern * intersection).astype(jnp.bfloat16)
        potential = (
            jnp.dot(x_mine, mixed, preferred_element_type=jnp.float32) * weights[None, :]
        ).astype(jnp.bfloat16)
        potential = potential.reshape(nsig, rows_mine, npoints)
        block_k = jnp.einsum(
            "mp,tkp->mtk",
            x_mine,
            lax.all_gather(potential, "rows", axis=1, tiled=True),
            preferred_element_type=jnp.float32,
        )
        block_k = block_k.reshape(nsig, rows_mine, nsig, block_size)
        totals = totals.at[blocks[:, None], :, blocks[None, :], :].add(
            block_k.transpose(0, 2, 1, 3)
        )
    return lax.psum_scatter(
        totals.reshape(nblocks, rows_mine, nbasis), "grid", scatter_dimension=2, tiled=True
    )


def solution(mesh):
    placed = (
        P(None, "rows", "grid"),
        P("grid", None, "rows", None),
        P("grid", None, None),
        P("grid", None),
        P("grid", None),
    )
    return jax.shard_map(
        body, mesh=mesh, in_specs=placed, out_specs=P(None, "rows", "grid"), check_vma=False
    )
```

profile of v0, /device:TPU:0, one launch (start us, length us, event | category | flops | bytes accessed | tf_op | source)
XLA Modules:
  0.0 572.5 jit_solution(16403228100501752769)
XLA Ops:
  10.5 57.3 %all-gather.8.cloned.1.call-done = bf16[32,32,4096]{2,1,0:T(8,128)(2,1)} async-done(((bf16[32,32,512]{2,1,0:T(8,128)(2,1)}), bf16[32,32,4096]{2,1,0:T(8,128)(2,1)}) %all-gather.8.cloned.1.call-update) | async-done | bytes 8388624 | tf_op jit(solution)/shard_map/all_gather | solution.py:14
  67.8 6.2 %gather_fusion.2 = bf16[16,32,4096]{2,1,0:T(8,128)(2,1)} fusion(bf16[32,32,4096]{2,1,0:T(8,128)(2,1)} %all-gather.8.cloned.1.call-done, s32[1024]{0:T(1024)S(1)} %pad_clamp_fusion), kind=kCustom, calls=%fused_computation.2.clone | custom fusion | bytes 8388672 | tf_op jit(solution)/shard_map/jit(_take)/gather | solution.py:18
  78.0 3.6 copy.23
  84.8 6.2 %gather_fusion = bf16[16,32,4096]{2,1,0:T(8,128)(2,1)} fusion(bf16[32,32,4096]{2,1,0:T(8,128)(2,1)} %all-gather.8.cloned.1.call-done, s32[1024]{0:T(1024)S(1)} %pad_clamp_fusion.1), kind=kCustom, calls=%fused_computation.clone | custom fusion | bytes 8388672 | tf_op jit(solution)/shard_map/jit(_take)/gather | solution.py:18
  94.9 3.6 copy.19
  98.5 4.4 gather_fusion.1
  102.9 12.2 %all-gather.16.cloned.1.call-done = bf16[1,16,128,512]{3,2,1,0:T(8,128)(2,1)} async-done(((bf16[1,16,32,512]{3,2,1,0:T(8,128)(2,1)}), bf16[1,16,128,512]{3,2,1,0:T(8,128)(2,1)}) %all-gather.16.cloned.1.call-update) | async-done | bytes 2097168 | tf_op jit(solution)/shard_map/all_gather | solution.py:25
  115.1 4.3 convolution_bitcast_fusion.2
  119.4 41.8 %all-gather.14.cloned.1.call-done = bf16[1,16,128,512]{3,2,1,0:T(8,128)(2,1)} async-done(((bf16[1,16,32,512]{3,2,1,0:T(8,128)(2,1)}), bf16[1,16,128,512]{3,2,1,0:T(8,128)(2,1)}) %all-gather.14.cloned.1.call-update) | async-done | bytes 2097168 | tf_op jit(solution)/shard_map/all_gather | solution.py:25
  161.2 4.9 convolution_bitcast_fusion.3
  166.9 84.3 %all-reduce.3.cloned.1.call-done = (f32[512,512]{0,1:T(8,128)}, f32[512,512]{0,1:T(8,128)}) async-done(((f32[512,512]{0,1:T(8,128)}, f32[512,512]{0,1:T(8,128)}), (f32[512,512]{0,1:T(8,128)}, f32[512,512]{0,1:T(8,128)})) %all-reduce.3.cloned.1.call-update) | async-done | bytes 2097168 | tf_op jit(solution)/shard_map/psum | solution.py:32
  257.6 41.0 %all-gather.10.cloned.1.call-done = bf16[16,128,512]{2,1,0:T(8,128)(2,1)} async-done(((bf16[16,32,512]{2,1,0:T(8,128)(2,1)}), bf16[16,128,512]{2,1,0:T(8,128)(2,1)}) %all-gather.10.cloned.1.call-update) | async-done | bytes 2097168 | tf_op jit(solution)/shard_map/all_gather | solution.py:45
  298.6 4.8 convolution_bitcast_fusion.1
  303.4 5.5 copy.20
  309.0 5.5 copy.21
  314.4 30.1 %all-gather.12.cloned.1.call-done = bf16[16,128,512]{2,1,0:T(8,128)(2,1)} async-done(((bf16[16,32,512]{2,1,0:T(8,128)(2,1)}), bf16[16,128,512]{2,1,0:T(8,128)(2,1)}) %all-gather.12.cloned.1.call-update) | async-done | bytes 2097168 | tf_op jit(solution)/shard_map/all_gather | solution.py:45
  344.5 4.8 convolution_bitcast_fusion
  349.3 5.5 copy.24
  354.8 5.5 copy.25
  360.3 7.9 %broadcast_in_dim.45 = f32[32,32,32,128]{3,1,2,0:T(8,128)} broadcast(f32[]{:T(128)} %constant.20.clone.1), dimensions={} | broadcast | bytes 16777220 | tf_op jit(solution)/shard_map/broadcast_in_dim | solution.py:15
  368.2 35.3 %scatter_fusion = f32[32,32,32,128]{3,1,2,0:T(8,128)} fusion(f32[32,32,32,128]{3,1,2,0:T(8,128)} %broadcast_in_dim.45, s32[256]{0:T(256)S(1)} %reshape.132, f32[256,32,128]{2,1,0:T(8,128)} %bitcast.123), kind=kCustom, calls=%fused_computation.4 | custom fusion | flops 1048576 | bytes 12584960 | tf_op jit(solution)/shard_map/scatter-add | solution.py:49
  403.5 35.3 %scatter_fusion.1 = f32[32,32,32,128]{3,1,2,0:T(8,128)} fusion(f32[32,32,32,128]{3,1,2,0:T(8,128)} %scatter_fusion, s32[256]{0:T(256)S(1)} %reshape.138, f32[256,32,128]{2,1,0:T(8,128)} %bitcast.124), kind=kCustom, calls=%fused_computation.5 | custom fusion | flops 1048576 | bytes 12584960 | tf_op jit(solution)/shard_map/scatter-add | solution.py:49
  438.9 11.7 %copy_bitcast_fusion = f32[32,32,4096]{2,1,0:T(8,128)} fusion(f32[32,32,32,128]{3,1,2,0:T(8,128)} %scatter_fusion.1), kind=kLoop, calls=%fused_computation.6 | loop fusion | bytes 33554432 | tf_op jit(solution)/shard_map/reshape | solution.py:53
  450.6 115.0 %reduce-scatter.2.cloned.1.call-done = f32[32,32,512]{2,1,0:T(8,128)} async-done(((f32[32,32,4096]{2,1,0:T(8,128)}), f32[32,32,512]{2,1,0:T(8,128)}) %reduce-scatter.2.cloned.1.call-update) | async-done | bytes 2097168 | tf_op jit(solution)/shard_map/reduce_scatter | solution.py:52
  (50 shorter events, 22.0 us)
Async XLA Ops:
  6.5 3.9 copy-start.4
  6.5 61.3 %all-gather.8.cloned.1.call-start = ((), (), s32[]{:S(2)}) async-start(), calls=%async_computation.1 | async-start | bytes 9437184 | tf_op jit(solution)/shard_map/all_gather | solution.py:14
  7.3 107.8 %all-gather.16.cloned.1.call-start = ((), (), s32[]{:S(2)}) async-start(), calls=%async_computation.6 | async-start | bytes 2621440 | tf_op jit(solution)/shard_map/all_gather | solution.py:25
  9.6 151.5 %all-gather.14.cloned.1.call-start = ((), (), s32[]{:S(2)}) async-start(), calls=%async_computation.5 | async-start | bytes 2621440 | tf_op jit(solution)/shard_map/all_gather | solution.py:25
  10.4 240.8 %all-reduce.3.cloned.1.call-start = ((), (), s32[]{:S(2)}) async-start(), calls=%async_computation.7 | async-start | bytes 4194304 | tf_op jit(solution)/shard_map/psum | solution.py:32
  98.5 16.6 %copy-start = (bf16[1,16,32,512]{3,2,1,0:T(8,128)(2,1)S(1)}, bf16[1,16,32,512]{3,2,1,0:T(8,128)(2,1)}, u32[]{:S(2)}) copy-start(bf16[1,16,32,512]{3,2,1,0:T(8,128)(2,1)} %get-tuple-element.13) | copy-start | bytes 1572868
  115.1 46.1 %copy-start.1 = (bf16[1,16,32,512]{3,2,1,0:T(8,128)(2,1)S(1)}, bf16[1,16,32,512]{3,2,1,0:T(8,128)(2,1)}, u32[]{:S(2)}) copy-start(bf16[1,16,32,512]{3,2,1,0:T(8,128)(2,1)} %get-tuple-element.14) | copy-start | bytes 1572868
  161.2 5.0 copy-start.2
  166.0 0.8 copy-start.3
  166.1 132.5 %all-gather.10.cloned.1.call-start = ((), (), s32[]{:S(2)}) async-start(), calls=%async_computation.2 | async-start | bytes 2621440 | tf_op jit(solution)/shard_map/all_gather | solution.py:45
  253.7 90.8 %all-gather.12.cloned.1.call-start = ((), (), s32[]{:S(2)}) async-start(), calls=%async_computation.3 | async-start | bytes 2621440 | tf_op jit(solution)/shard_map/all_gather | solution.py:45
  257.0 308.6 %reduce-scatter.2.cloned.1.call-start = ((), (), s32[]{:S(2)}) async-start(), calls=%async_computation.4 | async-start | bytes 18874368 | tf_op jit(solution)/shard_map/reduce_scatter | solution.py:52
Sparse Core Ops, SparseCore 0:
  9.2 58.5 all-gather.7
  69.4 45.6 all-gather.15
  116.7 44.4 all-gather.13
  166.2 84.9 all-reduce.2
  253.9 44.6 all-gather.9
  300.0 44.4 all-gather.11
  450.7 114.8 reduce-scatter.1
where the time goes:
time: 574 us; the launch traced here: 572 us
  waiting for transfers between devices  383 us (67%)
  other arithmetic  76.9 us (13%)
  local copies, waits for them, and re-layouts  74.4 us (13%)
  matrix products  23.9 us (4%)
  between operations  13.7 us (2%)
    reduce_scatter x1, waiting for transfers between devices, body(): lax.psum_scatter(totals.reshape(nblocks, rows_mine, nbasis), 'grid', scat...  115 us
    psum x1, waiting for transfers between devices, body(): intersection = lax.psum(intersection_part, 'rows')  84.3 us
    all_gather x2, waiting for transfers between devices, body(): lax.all_gather(potential, 'rows', axis=1, tiled=True)  71.1 us
    scatter-add x2, other arithmetic, body(): totals.at[blocks[:, None], :, blocks[None, :], :]  70.6 us
    all_gather x1, waiting for transfers between devices, body(): stripe = lax.all_gather(density, 'grid', axis=2, tiled=True)  57.3 us
    all_gather x2, waiting for transfers between devices, body(): lax.all_gather(local_values, 'rows', axis=1, tiled=True)  53.9 us
    gather x2, local copies, waits for them, and re-layouts, body(): jnp.take(stripe, blocks, axis=0)  12.4 us
    reshape x1, local copies, waits for them, and re-layouts, body(): totals.reshape(nblocks, rows_mine, nbasis)  11.7 us
  transfers between devices with their start and end apart: 7, of which 7 were waited for; matrix products, arithmetic and copies ran while one was open for 11% of the time, Pallas kernels for 0%

commit v1 on v0

--- a/solution.py
+++ b/solution.py
@@ -29,7 +29,11 @@
         intersection_part = lax.dot_general(
             x_mine, fmat, (((0,), (0,)), ((), ())), preferred_element_type=jnp.float32
         )
-        intersection = lax.psum(intersection_part, "rows")
+        intersection = intersection_part
+        for hop in (1, 2):
+            intersection = intersection + lax.ppermute(
+                intersection, "rows", [(dev, dev ^ hop) for dev in range(4)]
+            )
         places = grid_points[batch_index]
         weights = grid_weights[batch_index]
         diffs = places[:, :, None] - places[:, None, :]

time: 574 us -> 622 us (1.084)
  waiting for transfers between devices: 383 us -> 427 us
    ppermute x0 -> x4, waiting for transfers between devices: none -> 194 us  [body(): lax.ppermute(intersection, 'rows', [(dev, dev ^ hop) for dev in range(4)])]
    psum x1 -> x0, waiting for transfers between devices: 84.3 us -> none  [body(): intersection = lax.psum(intersection_part, 'rows')]
    all_gather x2, waiting for transfers between devices: 71.1 us -> 28.6 us  [body(): lax.all_gather(potential, 'rows', axis=1, tiled=True)]
    all_gather x2, waiting for transfers between devices: 53.9 us -> 30.3 us  [body(): lax.all_gather(local_values, 'rows', axis=1, tiled=True)]
  transfers between devices with their start and end apart: 7 -> 10, of which waited for: 7 -> 8; matrix products, arithmetic and copies ran while one was open for 11% -> 12% of each run, Pallas kernels for 0% -> 0%
where the time goes in v1:
time: 622 us; the launch traced here: 621 us
  waiting for transfers between devices  427 us (69%)
  other arithmetic  79.9 us (13%)
  local copies, waits for them, and re-layouts  75.3 us (12%)
  matrix products  23.6 us (4%)
  between operations  13.7 us (2%)
    ppermute x4, waiting for transfers between devices, body(): lax.ppermute(intersection, 'rows', [(dev, dev ^ hop) for dev in range(4)])  194 us
    reduce_scatter x1, waiting for transfers between devices, body(): lax.psum_scatter(totals.reshape(nblocks, rows_mine, nbasis), 'grid', scat...  115 us
    scatter-add x2, other arithmetic, body(): totals.at[blocks[:, None], :, blocks[None, :], :]  70.7 us
    all_gather x1, waiting for transfers between devices, body(): stripe = lax.all_gather(density, 'grid', axis=2, tiled=True)  57.4 us
    all_gather x2, waiting for transfers between devices, body(): lax.all_gather(local_values, 'rows', axis=1, tiled=True)  30.3 us
    all_gather x2, waiting for transfers between devices, body(): lax.all_gather(potential, 'rows', axis=1, tiled=True)  28.6 us
  transfers between devices with their start and end apart: 10, of which 8 were waited for; matrix products, arithmetic and copies ran while one was open for 12% of the time, Pallas kernels for 0%

profile of v1, /device:TPU:0, one launch (start us, length us, event | category | flops | bytes accessed | tf_op | source)
XLA Modules:
  0.0 620.8 jit_solution(16273809394280269792)
XLA Ops:
  10.4 57.4 %all-gather.8.cloned.1.call-done = bf16[32,32,4096]{2,1,0:T(8,128)(2,1)} async-done(((bf16[32,32,512]{2,1,0:T(8,128)(2,1)}), bf16[32,32,4096]{2,1,0:T(8,128)(2,1)}) %all-gather.8.cloned.1.call-update) | async-done | bytes 8388624 | tf_op jit(solution)/shard_map/all_gather | solution.py:14
  67.8 6.2 gather_fusion
  78.0 3.6 copy.19
  84.8 30.3 %all-gather.14.cloned.1.call-done = bf16[1,16,128,512]{3,2,1,0:T(8,128)(2,1)} async-done(((bf16[1,16,32,512]{3,2,1,0:T(8,128)(2,1)}), bf16[1,16,128,512]{3,2,1,0:T(8,128)(2,1)}) %all-gather.14.cloned.1.call-update) | async-done | bytes 2097168 | tf_op jit(solution)/shard_map/all_gather | solution.py:25
  115.1 4.2 convolution_bitcast_fusion.3
  119.5 58.5 %collective-permute-done = f32[512,512]{0,1:T(8,128)S(1)} collective-permute-done((f32[512,512]{0,1:T(8,128)}, f32[512,512]{0,1:T(8,128)S(1)}, u32[]{:S(2)}, u32[]{:S(2)}) %collective-permute-start) | collective-permute-done | bytes 1048608 | tf_op jit(solution)/shard_map/ppermute | solution.py:34
  181.3 6.3 %gather_fusion.2 = bf16[16,32,4096]{2,1,0:T(8,128)(2,1)} fusion(bf16[32,32,4096]{2,1,0:T(8,128)(2,1)} %all-gather.8.cloned.1.call-done, s32[1024]{0:T(1024)S(1)} %pad_clamp_fusion), kind=kCustom, calls=%fused_computation.2.clone | custom fusion | bytes 8388672 | tf_op jit(solution)/shard_map/jit(_take)/gather | solution.py:18
  187.5 38.7 %collective-permute-done.1 = f32[512,512]{0,1:T(8,128)} collective-permute-done((f32[512,512]{0,1:T(8,128)S(1)}, f32[512,512]{0,1:T(8,128)}, u32[]{:S(2)}, u32[]{:S(2)}) %collective-permute-start.1) | collective-permute-done | bytes 1048608 | tf_op jit(solution)/shard_map/ppermute | solution.py:34
  233.0 3.6 copy.23
  239.9 4.2 convolution_bitcast_fusion.2
  244.1 50.8 %collective-permute-done.2 = f32[512,512]{0,1:T(8,128)S(1)} collective-permute-done((f32[512,512]{0,1:T(8,128)}, f32[512,512]{0,1:T(8,128)S(1)}, u32[]{:S(2)}, u32[]{:S(2)}) %collective-permute-start.2) | collective-permute-done | bytes 1048608 | tf_op jit(solution)/shard_map/ppermute | solution.py:34
  298.7 46.2 %collective-permute-done.3 = f32[512,512]{0,1:T(8,128)} collective-permute-done((f32[512,512]{0,1:T(8,128)S(1)}, f32[512,512]{0,1:T(8,128)}, u32[]{:S(2)}, u32[]{:S(2)}) %collective-permute-start.3) | collective-permute-done | bytes 1048608 | tf_op jit(solution)/shard_map/ppermute | solution.py:34
  348.4 4.8 convolution_bitcast_fusion.1
  353.2 5.6 copy.20
  358.8 5.4 copy.21
  364.2 28.6 %all-gather.12.cloned.1.call-done = bf16[16,128,512]{2,1,0:T(8,128)(2,1)} async-done(((bf16[16,32,512]{2,1,0:T(8,128)(2,1)}), bf16[16,128,512]{2,1,0:T(8,128)(2,1)}) %all-gather.12.cloned.1.call-update) | async-done | bytes 2097168 | tf_op jit(solution)/shard_map/all_gather | solution.py:49
  392.9 4.8 convolution_bitcast_fusion
  397.7 5.5 copy.24
  403.2 5.5 copy.25
  408.7 7.9 %broadcast_in_dim.45 = f32[32,32,32,128]{3,1,2,0:T(8,128)} broadcast(f32[]{:T(128)} %constant.20.clone.1), dimensions={} | broadcast | bytes 16777220 | tf_op jit(solution)/shard_map/broadcast_in_dim | solution.py:15
  416.6 35.3 %scatter_fusion = f32[32,32,32,128]{3,1,2,0:T(8,128)} fusion(f32[32,32,32,128]{3,1,2,0:T(8,128)} %broadcast_in_dim.45, s32[256]{0:T(256)S(1)} %reshape.132, f32[256,32,128]{2,1,0:T(8,128)} %bitcast.123), kind=kCustom, calls=%fused_computation.4 | custom fusion | flops 1048576 | bytes 12584960 | tf_op jit(solution)/shard_map/scatter-add | solution.py:53
  451.9 35.4 %scatter_fusion.1 = f32[32,32,32,128]{3,1,2,0:T(8,128)} fusion(f32[32,32,32,128]{3,1,2,0:T(8,128)} %scatter_fusion, s32[256]{0:T(256)S(1)} %reshape.138, f32[256,32,128]{2,1,0:T(8,128)} %bitcast.124), kind=kCustom, calls=%fused_computation.5 | custom fusion | flops 1048576 | bytes 12584960 | tf_op jit(solution)/shard_map/scatter-add | solution.py:53
  487.3 11.7 %copy_bitcast_fusion = f32[32,32,4096]{2,1,0:T(8,128)} fusion(f32[32,32,32,128]{3,1,2,0:T(8,128)} %scatter_fusion.1), kind=kLoop, calls=%fused_computation.6 | loop fusion | bytes 33554432 | tf_op jit(solution)/shard_map/reshape | solution.py:57
  499.0 115.0 %reduce-scatter.2.cloned.1.call-done = f32[32,32,512]{2,1,0:T(8,128)} async-done(((f32[32,32,4096]{2,1,0:T(8,128)}), f32[32,32,512]{2,1,0:T(8,128)}) %reduce-scatter.2.cloned.1.call-update) | async-done | bytes 2097168 | tf_op jit(solution)/shard_map/reduce_scatter | solution.py:56
  (58 shorter events, 31.7 us)
Async XLA Ops:
  6.5 3.9 copy-start.5
  6.5 61.3 %all-gather.8.cloned.1.call-start = ((), (), s32[]{:S(2)}) async-start(), calls=%async_computation.1 | async-start | bytes 9437184 | tf_op jit(solution)/shard_map/all_gather | solution.py:14
  7.3 107.8 %all-gather.14.cloned.1.call-start = ((), (), s32[]{:S(2)}) async-start(), calls=%async_computation.5 | async-start | bytes 2621440 | tf_op jit(solution)/shard_map/all_gather | solution.py:25
  9.6 230.3 %all-gather.16.cloned.1.call-start = ((), (), s32[]{:S(2)}) async-start(), calls=%async_computation.6 | async-start | bytes 2621440 | tf_op jit(solution)/shard_map/all_gather | solution.py:25
  10.3 338.0 %all-gather.10.cloned.1.call-start = ((), (), s32[]{:S(2)}) async-start(), calls=%async_computation.2 | async-start | bytes 2621440 | tf_op jit(solution)/shard_map/all_gather | solution.py:49
  81.6 33.5 %copy-start.1 = (bf16[1,16,32,512]{3,2,1,0:T(8,128)(2,1)S(1)}, bf16[1,16,32,512]{3,2,1,0:T(8,128)(2,1)}, u32[]{:S(2)}) copy-start(bf16[1,16,32,512]{3,2,1,0:T(8,128)(2,1)} %get-tuple-element.12) | copy-start | bytes 1572868
  115.1 64.4 %copy-start.3 = (f32[2,3,512]{2,0,1:T(2,128)S(1)}, f32[2,3,512]{2,0,1:T(2,128)}, u32[]{:S(2)}) copy-start(f32[2,3,512]{2,0,1:T(2,128)} %param.11) | copy-start | bytes 36868
  119.3 61.9 %copy-start.4 = (f32[2,512]{1,0:T(2,128)S(1)}, f32[2,512]{1,0:T(2,128)}, u32[]{:S(2)}) copy-start(f32[2,512]{1,0:T(2,128)} %param.12) | copy-start | bytes 12292
  119.3 58.7 %collective-permute-start = (f32[512,512]{0,1:T(8,128)}, f32[512,512]{0,1:T(8,128)S(1)}, u32[]{:S(2)}, u32[]{:S(2)}) collective-permute-start(f32[512,512]{0,1:T(8,128)} %convolution_bitcast_fusion.3), channel_id=1, source_target_pairs={{0,1},{1,0},{2,3},{3,2},{4,5},{5,4},{6,7},{7,6},{8,9},{9,8},{10,11... | collective-permute-start | bytes 3145736 | tf_op jit(solution)/shard_map/ppermute | solution.py:34
  179.4 46.8 %collective-permute-start.1 = (f32[512,512]{0,1:T(8,128)S(1)}, f32[512,512]{0,1:T(8,128)}, u32[]{:S(2)}, u32[]{:S(2)}) collective-permute-start(f32[512,512]{0,1:T(8,128)S(1)} %add.55), channel_id=1, source_target_pairs={{0,2},{1,3},{2,0},{3,1},{4,6},{5,7},{6,4},{7,5},{8,10},{9,11},{10,... | collective-permute-start | bytes 3145736 | tf_op jit(solution)/shard_map/ppermute | solution.py:34
  181.3 45.0 %copy-start.2 = (f32[512,512]{0,1:T(8,128)S(1)}, f32[512,512]{0,1:T(8,128)}, u32[]{:S(2)}) copy-start(f32[512,512]{0,1:T(8,128)} %copy.18) | copy-start | bytes 3145732
  228.8 164.0 %all-gather.12.cloned.1.call-start = ((), (), s32[]{:S(2)}) async-start(), calls=%async_computation.3 | async-start | bytes 2621440 | tf_op jit(solution)/shard_map/all_gather | solution.py:49
  236.6 3.3 copy-start
  244.1 50.8 %collective-permute-start.2 = (f32[512,512]{0,1:T(8,128)}, f32[512,512]{0,1:T(8,128)S(1)}, u32[]{:S(2)}, u32[]{:S(2)}) collective-permute-start(f32[512,512]{0,1:T(8,128)} %convolution_bitcast_fusion.2), channel_id=1, source_target_pairs={{0,1},{1,0},{2,3},{3,2},{4,5},{5,4},{6,7},{7,6},{8,9},{9,8},{10,11... | collective-permute-start | bytes 3145736 | tf_op jit(solution)/shard_map/ppermute | solution.py:34
  296.4 48.5 %collective-permute-start.3 = (f32[512,512]{0,1:T(8,128)S(1)}, f32[512,512]{0,1:T(8,128)}, u32[]{:S(2)}, u32[]{:S(2)}) collective-permute-start(f32[512,512]{0,1:T(8,128)S(1)} %add.60), channel_id=1, source_target_pairs={{0,2},{1,3},{2,0},{3,1},{4,6},{5,7},{6,4},{7,5},{8,10},{9,11},{10,... | collective-permute-start | bytes 3145736 | tf_op jit(solution)/shard_map/ppermute | solution.py:34
  347.7 266.2 %reduce-scatter.2.cloned.1.call-start = ((), (), s32[]{:S(2)}) async-start(), calls=%async_computation.4 | async-start | bytes 18874368 | tf_op jit(solution)/shard_map/reduce_scatter | solution.py:56
Sparse Core Ops, SparseCore 0:
  9.2 58.5 all-gather.7
  69.4 45.6 all-gather.13
  116.7 60.1 all-gather.15
  228.9 64.0 all-gather.9
  347.9 44.9 all-gather.11
  499.1 114.8 reduce-scatter.1
